TPU v7x, 32 devices: a whole 2x2x4 slice. The times are simulated.
32 devices in a mesh: dp: 8 (over z, y), tensor: 4 (over x, core).
Axes of the slice: x: 2, y: 2, z: 4, core: 2. Of those that a mesh axis runs over, the one named last changes fastest.
Arguments:
- attn_out: bfloat16 [2048, 4096], P('dp', 'tensor'), may hold values from -6 to 6
- w_blocks: bfloat16 [4096, 8192], P('tensor', 'dp'), may hold values from -0.09375 to 0.09375
- w_scales: float32 [32, 8192], P('tensor', 'dp'), may hold values from 0.5 to 2
- residual: bfloat16 [2048, 8192], P('dp')
- gain: float32 [8192], P('tensor'), may hold values from 0.5 to 1.5
Outputs:
- hidden: bfloat16 [2048, 8192], P('dp', 'tensor')
- normed: bfloat16 [2048, 8192], P('dp', 'tensor')
All inputs are finite; a program needn't handle non-finite values.
Results may differ from a plain program's by a relative error of at most 0.014.
Values may be sent and summed in bfloat16 or wider, within the bound.
A program may use at most 128 MiB of HBM per device.

v0:
```python
import jax
import jax.numpy as jnp
from jax import lax
from jax.sharding import PartitionSpec as P

BLOCK = 128


def dequantize(blocks, scales):
    rows, cols = blocks.shape
    shaped = blocks.astype(jnp.float32).reshape(rows // BLOCK, BLOCK, cols)
    return (shaped * scales[:, None, :]).reshape(rows, cols).astype(jnp.bfloat16)


def on_device(attn_out, w_blocks, w_scales, residual, gain):
    everyone = lax.all_gather(attn_out, "dp", axis=0, tiled=True)
    local_cols = jnp.dot(
        everyone, dequantize(w_blocks, w_scales), preferred_element_type=jnp.float32
    )
    partial_value = lax.all_to_all(
        local_cols.astype(jnp.bfloat16), "dp", split_axis=0, concat_axis=1, tiled=True
    ).astype(local_cols.dtype)
    wide_cols = residual.shape[1]
    my_cols = gain.shape[0]
    offset = lax.axis_index("tensor") * my_cols
    total = lax.psum(partial_value.astype(jnp.bfloat16), "tensor").astype(jnp.float32)
    hidden_full = (residual.astype(jnp.float32) + total).astype(jnp.bfloat16)
    widened = hidden_full.astype(jnp.float32)
    mean_square = jnp.sum(widened * widened, axis=1, keepdims=True) / wide_cols
    mine = lax.dynamic_slice_in_dim(hidden_full, offset, my_cols, 1)
    normed = (mine.astype(jnp.float32) * gain[None, :] * lax.rsqrt(mean_square + 1e-05)).astype(
        jnp.bfloat16
    )
    return (mine, normed)


def solution(mesh):
    return jax.shard_map(
        on_device,
        mesh=mesh,
        in_specs=(
            P("dp", "tensor"),
            P("tensor", "dp"),
            P("tensor", "dp"),
            P("dp", None),
            P("tensor"),
        ),
        out_specs=(P("dp", "tensor"), P("dp", "tensor")),
        check_vma=False,
    )
```

profile of v0, /device:TPU:0, one launch (start us, length us, event | category | flops | bytes accessed | tf_op | source)
XLA Modules:
  0.0 293.9 jit_solution(12024145223568308483)
XLA Ops:
  7.2 0.0 all-gather.2.cloned.1.call-start
  7.2 0.7 all-gather.2.cloned.1.call-update
  7.9 0.0 all-reduce.2.cloned.1.call-start
  7.9 2.2 fusion
  10.1 75.5 %all-gather.2.cloned.1.call-done = bf16[2048,1024]{1,0:T(8,128)(2,1)} async-done(((bf16[256,1024]{1,0:T(8,128)(2,1)}), bf16[2048,1024]{1,0:T(8,128)(2,1)}) %all-gather.2.cloned.1.call-update) | async-done | bytes 4194320 | tf_op jit(solution)/shard_map/all_gather | solution.py:16
  85.6 7.0 %convolution_convert_fusion = bf16[1024,2048]{1,0:T(8,128)(2,1)S(1)} fusion(bf16[1024,1024]{1,0:T(8,128)(2,1)S(1)} %fusion, bf16[2048,1024]{1,0:T(8,128)(2,1)} %all-gather.2.cloned.1.call-done), kind=kOutput, calls=%fused_computation.5 | convolution fusion | flops 4297064448 | bytes 10485760 | tf_op jit(solution)/shard_map/dot_general | solution.py:17
  92.7 0.3 copy.12
  93.0 96.4 %all_to_all.19 = bf16[8,256,1024]{1,2,0:T(8,128)(2,1)} all-to-all(bf16[8,256,1024]{1,2,0:T(8,128)(2,1)S(1)} %bitcast.14), channel_id=1, replica_groups=mesh['dp'=8,'tensor'=4] {'dp'}, dimensions={0} | all-to-all | bytes 8388608 | tf_op jit(solution)/shard_map/all_to_all | solution.py:20
  189.4 6.4 %copy.9 = bf16[256,8192]{1,0:T(8,128)(2,1)} copy(bf16[256,8192]{0,1:T(8,128)(2,1)} %bitcast.15) | data formatting | bytes 8388608 | tf_op jit(solution)/shard_map/all_to_all | solution.py:20
  195.7 0.0 all-reduce.2.cloned.1.call-update
  195.8 0.0 copy-start
  195.8 84.3 %all-reduce.2.cloned.1.call-done = bf16[256,8192]{1,0:T(8,128)(2,1)} async-done(((bf16[256,8192]{1,0:T(8,128)(2,1)}), bf16[256,8192]{1,0:T(8,128)(2,1)}) %all-reduce.2.cloned.1.call-update) | async-done | bytes 4194320 | tf_op jit(solution)/shard_map/psum | solution.py:26
  280.1 5.4 %multiply_reduce_fusion = (f32[256]{0:T(256)S(1)}, bf16[256,8192]{1,0:T(8,128)(2,1)S(1)}) fusion(bf16[256,8192]{1,0:T(8,128)(2,1)} %all-reduce.2.cloned.1.call-done, bf16[256,8192]{1,0:T(8,128)(2,1)} %param.8), kind=kLoop, calls=%fused_computation | loop fusion | flops 14679808 | bytes 12583936 | tf_op jit(solution)/shard_map/reduce_sum | solution.py:29
  285.5 0.0 copy-done
  285.5 1.6 multiply_convert_fusion
  (1 shorter events, 0.0 us)
Async XLA Ops:
  7.2 78.5 %all-gather.2.cloned.1.call-start = ((), (), s32[]{:S(2)}) async-start(), calls=%async_computation.1 | async-start | bytes 4718592 | tf_op jit(solution)/shard_map/all_gather | solution.py:16
  7.9 272.2 %all-reduce.2.cloned.1.call-start = ((), (), s32[]{:S(2)}) async-start(), calls=%async_computation.2 | async-start | bytes 8388608 | tf_op jit(solution)/shard_map/psum | solution.py:26
  195.8 89.7 %copy-start = (f32[2048]{0:T(1024)S(1)}, f32[2048]{0:T(1024)}, u32[]{:S(2)}) copy-start(f32[2048]{0:T(1024)} %param.9) | copy-start | bytes 24580
Sparse Core Ops, SparseCore 0:
  10.1 75.5 all-gather.1
  195.9 84.1 all-reduce.1
where the time goes:
time: 294 us
  waiting for transfers between devices  161 us (55%)
  blocking collectives  96.4 us (33%)
  between operations  14.1 us (5%)
  other arithmetic  9.16 us (3%)
  matrix products  7.02 us (2%)
  local copies, waits for them, and re-layouts  6.65 us (2%)
    all_to_all x1, blocking collectives, on_device(): lax.all_to_all(local_cols.astype(jnp.bfloat16), 'dp', split_axis=0, conca...  96.4 us
    psum x1, waiting for transfers between devices, on_device(): lax.psum(partial_value.astype(jnp.bfloat16), 'tensor').astype(jnp.float32)  84.3 us
    all_gather x1, waiting for transfers between devices, on_device(): everyone = lax.all_gather(attn_out, 'dp', axis=0, tiled=True)  75.5 us
    dot_general x1, matrix products, on_device(): jnp.dot(everyone, dequantize(w_blocks, w_scales), preferred_element_type=...  7.02 us
    all_to_all x2, local copies, waits for them, and re-layouts, on_device(): lax.all_to_all(local_cols.astype(jnp.bfloat16), 'dp', split_axis=0, conca...  6.64 us
  transfers between devices with their start and end apart: 2, of which 2 were waited for; matrix products, arithmetic and copies ran while one was open for 1% of the time, Pallas kernels for 0%

commit v1 on v0

--- a/solution.py
+++ b/solution.py
@@ -4,6 +4,17 @@
 from jax.sharding import PartitionSpec as P
 
 BLOCK = 128
+
+
+def pass_along(x, axis, dim):
+    size = lax.axis_size(axis)
+    forward = [(i, (i + 1) % size) for i in range(size)]
+    parts = [x]
+    for far in range(1, size):
+        parts = [lax.ppermute(parts[0], axis, forward), *parts]
+    out = jnp.concatenate(parts, axis=dim)
+    shift = (lax.axis_index(axis) + 1) * parts[-1].shape[dim]
+    return jnp.roll(out, shift, axis=dim)
 
 
 def dequantize(blocks, scales):
@@ -13,7 +24,7 @@
 
 
 def on_device(attn_out, w_blocks, w_scales, residual, gain):
-    everyone = lax.all_gather(attn_out, "dp", axis=0, tiled=True)
+    everyone = pass_along(attn_out, "dp", 0)
     local_cols = jnp.dot(
         everyone, dequantize(w_blocks, w_scales), preferred_element_type=jnp.float32
     )

time: 294 us -> 308 us (1.048)
  waiting for transfers between devices: 161 us -> 179 us
  blocking collectives: 96.4 us -> 89.9 us
    ppermute x0 -> x7, waiting for transfers between devices: none -> 95.7 us  [pass_along(): parts = [lax.ppermute(parts[0], axis, forward), *parts]]
    all_gather x1 -> x0, waiting for transfers between devices: 75.5 us -> none  [on_device(): everyone = lax.all_gather(attn_out, 'dp', axis=0, tiled=True)]
    all_to_all x1, blocking collectives: 96.4 us -> 89.9 us  [on_device(): lax.all_to_all(local_cols.astype(jnp.bfloat16), 'dp', split_axis=0, conca...]
    unnamed x2 -> x19, local copies, waits for them, and re-layouts: 0.01 us -> 4.72 us
    all_to_all x2 -> x1, local copies, waits for them, and re-layouts: 6.64 us -> 2.42 us  [on_device(): lax.all_to_all(local_cols.astype(jnp.bfloat16), 'dp', split_axis=0, conca...]
  transfers between devices with their start and end apart: 2 -> 8, of which waited for: 2 -> 8; matrix products, arithmetic and copies ran while one was open for 1% -> 1% of each run, Pallas kernels for 0% -> 0%
where the time goes in v1:
time: 308 us
  waiting for transfers between devices  179 us (58%)
  blocking collectives  89.9 us (29%)
  between operations  14.2 us (5%)
  other arithmetic  9.13 us (3%)
  local copies, waits for them, and re-layouts  7.17 us (2%)
  matrix products  4.73 us (2%)
  starting transfers between devices  3.1 us (1%)
    ppermute x7, waiting for transfers between devices, pass_along(): parts = [lax.ppermute(parts[0], axis, forward), *parts]  95.7 us
    all_to_all x1, blocking collectives, on_device(): lax.all_to_all(local_cols.astype(jnp.bfloat16), 'dp', split_axis=0, conca...  89.9 us
    psum x1, waiting for transfers between devices, on_device(): lax.psum(partial_value.astype(jnp.bfloat16), 'tensor').astype(jnp.float32)  83.7 us
  transfers between devices with their start and end apart: 8, of which 8 were waited for; matrix products, arithmetic and copies ran while one was open for 1% of the time, Pallas kernels for 0%

profile of v1, /device:TPU:0, one launch (start us, length us, event | category | flops | bytes accessed | tf_op | source)
XLA Modules:
  0.0 307.7 jit_solution(11828250418955959834)
XLA Ops:
  7.2 0.0 copy-start
  7.2 0.0 all-reduce.2.cloned.1.call-start
  7.2 3.0 collective-permute-start
  10.3 15.2 %collective-permute-done = bf16[256,1024]{1,0:T(8,128)(2,1)S(1)} collective-permute-done((bf16[256,1024]{1,0:T(8,128)(2,1)}, bf16[256,1024]{1,0:T(8,128)(2,1)S(1)}, u32[]{:S(2)}, u32[]{:S(2)}) %collective-permute-start) | collective-permute-done | bytes 524320 | tf_op jit(solution)/shard_map/ppermute | solution.py:14
  25.4 0.0 collective-permute-start.1
  25.4 15.8 %collective-permute-done.1 = bf16[256,1024]{1,0:T(8,128)(2,1)S(1)} collective-permute-done((bf16[256,1024]{1,0:T(8,128)(2,1)S(1)}, bf16[256,1024]{1,0:T(8,128)(2,1)S(1)}, u32[]{:S(2)}, u32[]{:S(2)}) %collective-permute-start.1) | collective-permute-done | bytes 524320 | tf_op jit(solution)/shard_map/ppermute | solution.py:14
  41.2 0.0 collective-permute-start.2
  41.2 14.9 %collective-permute-done.2 = bf16[256,1024]{1,0:T(8,128)(2,1)S(1)} collective-permute-done((bf16[256,1024]{1,0:T(8,128)(2,1)S(1)}, bf16[256,1024]{1,0:T(8,128)(2,1)S(1)}, u32[]{:S(2)}, u32[]{:S(2)}) %collective-permute-start.2) | collective-permute-done | bytes 524320 | tf_op jit(solution)/shard_map/ppermute | solution.py:14
  56.2 0.0 collective-permute-start.3
  56.2 14.1 %collective-permute-done.3 = bf16[256,1024]{1,0:T(8,128)(2,1)S(1)} collective-permute-done((bf16[256,1024]{1,0:T(8,128)(2,1)S(1)}, bf16[256,1024]{1,0:T(8,128)(2,1)S(1)}, u32[]{:S(2)}, u32[]{:S(2)}) %collective-permute-start.3) | collective-permute-done | bytes 524320 | tf_op jit(solution)/shard_map/ppermute | solution.py:14
  70.2 0.0 collective-permute-start.4
  70.2 13.2 %collective-permute-done.4 = bf16[256,1024]{1,0:T(8,128)(2,1)S(1)} collective-permute-done((bf16[256,1024]{1,0:T(8,128)(2,1)S(1)}, bf16[256,1024]{1,0:T(8,128)(2,1)S(1)}, u32[]{:S(2)}, u32[]{:S(2)}) %collective-permute-start.4) | collective-permute-done | bytes 524320 | tf_op jit(solution)/shard_map/ppermute | solution.py:14
  83.4 0.0 collective-permute-start.5
  83.5 12.5 %collective-permute-done.5 = bf16[256,1024]{1,0:T(8,128)(2,1)} collective-permute-done((bf16[256,1024]{1,0:T(8,128)(2,1)S(1)}, bf16[256,1024]{1,0:T(8,128)(2,1)}, u32[]{:S(2)}, u32[]{:S(2)}) %collective-permute-start.5) | collective-permute-done | bytes 524320 | tf_op jit(solution)/shard_map/ppermute | solution.py:14
  95.9 0.0 collective-permute-start.6
  95.9 2.1 fusion
  98.1 10.0 %collective-permute-done.6 = bf16[256,1024]{1,0:T(8,128)(2,1)} collective-permute-done((bf16[256,1024]{1,0:T(8,128)(2,1)}, bf16[256,1024]{1,0:T(8,128)(2,1)}, u32[]{:S(2)}, u32[]{:S(2)}) %collective-permute-start.6) | collective-permute-done | bytes 524320 | tf_op jit(solution)/shard_map/ppermute | solution.py:14
  108.1 1.1 constant_dynamic-update-slice_fusion.15
  109.2 1.1 constant_dynamic-update-slice_fusion.14
  110.5 0.0 copy-done
  110.5 1.1 constant_dynamic-update-slice_fusion.7
  111.6 1.1 constant_dynamic-update-slice_fusion.6
  113.0 4.7 %fusion.3 = bf16[2048,1024]{1,0:T(8,128)(2,1)S(1)} fusion(bf16[1024,1024]{1,0:T(8,128)(2,1)S(1)} %fusion, bf16[4096,1024]{1,0:T(8,128)(2,1)S(1)} %constant_dynamic-update-slice_fusion, s32[]{:T(128)S(6)} %select_n.17), kind=kOutput, calls=%fused_computation.6 | convolution fusion | flops 4297064448 | bytes 10485764 | tf_op jit(solution)/shard_map/dot_general | solution.py:28
  117.7 89.9 %all_to_all.19 = bf16[8,256,1024]{2,1,0:T(8,128)(2,1)S(1)} all-to-all(bf16[8,256,1024]{2,1,0:T(8,128)(2,1)S(1)} %bitcast.11), channel_id=1, replica_groups=mesh['dp'=8,'tensor'=4] {'dp'}, dimensions={0} | all-to-all | bytes 8388608 | tf_op jit(solution)/shard_map/all_to_all | solution.py:31
  207.6 2.4 copy.8
  210.1 0.0 copy-start.1
  210.1 0.0 all-reduce.2.cloned.1.call-update
  210.1 83.7 %all-reduce.2.cloned.1.call-done = bf16[256,8192]{1,0:T(8,128)(2,1)} async-done(((bf16[256,8192]{1,0:T(8,128)(2,1)}), bf16[256,8192]{1,0:T(8,128)(2,1)}) %all-reduce.2.cloned.1.call-update) | async-done | bytes 4194320 | tf_op jit(solution)/shard_map/psum | solution.py:37
  293.8 5.4 %multiply_reduce_fusion = (f32[256]{0:T(256)S(1)}, bf16[256,8192]{1,0:T(8,128)(2,1)S(1)}) fusion(bf16[256,8192]{1,0:T(8,128)(2,1)} %all-reduce.2.cloned.1.call-done, bf16[256,8192]{1,0:T(8,128)(2,1)} %param.8), kind=kLoop, calls=%fused_computation | loop fusion | flops 14679808 | bytes 12583936 | tf_op jit(solution)/shard_map/reduce_sum | solution.py:40
  299.2 0.0 copy-done.1
  299.2 1.6 multiply_convert_fusion
  (13 shorter events, 0.4 us)
Async XLA Ops:
  7.2 103.3 %copy-start = (bf16[256,1024]{1,0:T(8,128)(2,1)S(1)}, bf16[256,1024]{1,0:T(8,128)(2,1)}, u32[]{:S(2)}) copy-start(bf16[256,1024]{1,0:T(8,128)(2,1)} %param.5) | copy-start | bytes 1572868
  7.2 286.6 %all-reduce.2.cloned.1.call-start = ((), (), s32[]{:S(2)}) async-start(), calls=%async_computation.1 | async-start | bytes 8388608 | tf_op jit(solution)/shard_map/psum | solution.py:37
  7.2 18.2 %collective-permute-start = (bf16[256,1024]{1,0:T(8,128)(2,1)}, bf16[256,1024]{1,0:T(8,128)(2,1)S(1)}, u32[]{:S(2)}, u32[]{:S(2)}) collective-permute-start(bf16[256,1024]{1,0:T(8,128)(2,1)} %param.5), channel_id=1, source_target_pairs={{0,4},{4,8},{8,12},{12,16},{16,20},{20,24},{24,28},{28,0},{1,5},{5... | collective-permute-start | bytes 1572872 | tf_op jit(solution)/shard_map/ppermute | solution.py:14
  25.4 15.8 %collective-permute-start.1 = (bf16[256,1024]{1,0:T(8,128)(2,1)S(1)}, bf16[256,1024]{1,0:T(8,128)(2,1)S(1)}, u32[]{:S(2)}, u32[]{:S(2)}) collective-permute-start(bf16[256,1024]{1,0:T(8,128)(2,1)S(1)} %collective-permute-done), channel_id=1, source_target_pairs={{0,4},{4,8},{8,12},{12,16},{16,20},{20,24},{24,28},{28,0},{1,5},{5... | collective-permute-start | bytes 1572872 | tf_op jit(solution)/shard_map/ppermute | solution.py:14
  41.2 14.9 %collective-permute-start.2 = (bf16[256,1024]{1,0:T(8,128)(2,1)S(1)}, bf16[256,1024]{1,0:T(8,128)(2,1)S(1)}, u32[]{:S(2)}, u32[]{:S(2)}) collective-permute-start(bf16[256,1024]{1,0:T(8,128)(2,1)S(1)} %collective-permute-done.1), channel_id=1, source_target_pairs={{0,4},{4,8},{8,12},{12,16},{16,20},{20,24},{24,28},{28,0},{1,5},{5... | collective-permute-start | bytes 1572872 | tf_op jit(solution)/shard_map/ppermute | solution.py:14
  56.2 14.1 %collective-permute-start.3 = (bf16[256,1024]{1,0:T(8,128)(2,1)S(1)}, bf16[256,1024]{1,0:T(8,128)(2,1)S(1)}, u32[]{:S(2)}, u32[]{:S(2)}) collective-permute-start(bf16[256,1024]{1,0:T(8,128)(2,1)S(1)} %collective-permute-done.2), channel_id=1, source_target_pairs={{0,4},{4,8},{8,12},{12,16},{16,20},{20,24},{24,28},{28,0},{1,5},{5... | collective-permute-start | bytes 1572872 | tf_op jit(solution)/shard_map/ppermute | solution.py:14
  70.2 13.2 %collective-permute-start.4 = (bf16[256,1024]{1,0:T(8,128)(2,1)S(1)}, bf16[256,1024]{1,0:T(8,128)(2,1)S(1)}, u32[]{:S(2)}, u32[]{:S(2)}) collective-permute-start(bf16[256,1024]{1,0:T(8,128)(2,1)S(1)} %collective-permute-done.3), channel_id=1, source_target_pairs={{0,4},{4,8},{8,12},{12,16},{16,20},{20,24},{24,28},{28,0},{1,5},{5... | collective-permute-start | bytes 1572872 | tf_op jit(solution)/shard_map/ppermute | solution.py:14
  83.4 12.5 %collective-permute-start.5 = (bf16[256,1024]{1,0:T(8,128)(2,1)S(1)}, bf16[256,1024]{1,0:T(8,128)(2,1)}, u32[]{:S(2)}, u32[]{:S(2)}) collective-permute-start(bf16[256,1024]{1,0:T(8,128)(2,1)S(1)} %collective-permute-done.4), channel_id=1, source_target_pairs={{0,4},{4,8},{8,12},{12,16},{16,20},{20,24},{24,28},{28,0},{1,5},{5... | collective-permute-start | bytes 1572872 | tf_op jit(solution)/shard_map/ppermute | solution.py:14
  95.9 12.2 %collective-permute-start.6 = (bf16[256,1024]{1,0:T(8,128)(2,1)}, bf16[256,1024]{1,0:T(8,128)(2,1)}, u32[]{:S(2)}, u32[]{:S(2)}) collective-permute-start(bf16[256,1024]{1,0:T(8,128)(2,1)} %collective-permute-done.5), channel_id=1, source_target_pairs={{0,4},{4,8},{8,12},{12,16},{16,20},{20,24},{24,28},{28,0},{1,5},{5... | collective-permute-start | bytes 1572872 | tf_op jit(solution)/shard_map/ppermute | solution.py:14
  210.1 89.1 %copy-start.1 = (f32[2048]{0:T(1024)S(1)}, f32[2048]{0:T(1024)}, u32[]{:S(2)}) copy-start(f32[2048]{0:T(1024)} %param.9) | copy-start | bytes 24580
Sparse Core Ops, SparseCore 0:
  210.2 83.5 all-reduce.1
